TPU v7x, 128 devices: a whole 4x4x4 slice. The times are simulated.
128 devices in a mesh: row: 16 (over y, z), col: 8 (over x, core).
Axes of the slice: x: 4, y: 4, z: 4, core: 2. Of those that a mesh axis runs over, the one named last changes fastest.
Arguments:
- new_dosage: float32 [8192, 1024], P(('col', 'row')), may hold values from 0 to 2
- old_dosage: float32 [32768, 1024], P(('row', 'col')), may hold values from 0 to 2
- grm: bfloat16 [32768, 8192], P('row', 'col'), may hold values from -1.5 to 1.5
- counts: int32 [16], P('col'), may hold values from 256 to 512
- affected: int32 [64, 16], P('row', 'col'), may hold values from 0 to 1, as said below
Outputs:
- updated: bfloat16 [32768, 8192], P('row', 'col')
Inputs may be any that keep to these rules, and one draw needn't show every extreme that they name: `affected`: the density of marked tile pairs differs from one tile of new samples to the next.
All inputs are finite; a program needn't handle non-finite values.
Results may differ from a plain program's by a relative error of at most 0.00115.
Values may be sent and summed in bfloat16 or wider, within the bound.
A program may use at most 128 MiB of HBM per device.

v0:
```python
import jax
import jax.numpy as jnp
from jax import lax
from jax.sharding import Mesh
from jax.sharding import PartitionSpec as P

TILE = 512
ROW = ("row_0", "row_1")
COL = ("col_0", "col_1")
ROW_COL = ("row_0", "row_1", "col_0", "col_1")
COL_ROW = ("col_0", "col_1", "row_0", "row_1")


def one_axis_at_a_time(shard, axes):
    for axis in axes:
        shard = lax.psum(shard, axis)
    return shard


def sent_to_all(shard, axis):
    length = lax.axis_size(axis)
    return lax.all_to_all(
        jnp.broadcast_to(shard[None], (length, *shard.shape)), axis, 0, 0, tiled=True
    )


def joined_along(blocks, dim):
    lengths = list(blocks.shape[1:])
    lengths[dim] *= blocks.shape[0]
    return jnp.moveaxis(blocks, 0, dim).reshape(lengths)


def collect(shard, axis, dim):
    blocks = sent_to_all(shard, axis)
    return joined_along(blocks, dim)


def on_device(new_dosage, old_dosage, grm, counts, affected):
    devices = lax.axis_size(ROW) * lax.axis_size(COL)
    totals = one_axis_at_a_time(jnp.sum(old_dosage, axis=0), ROW_COL)
    doubled = totals / (old_dosage.shape[0] * devices)
    spread = jnp.sqrt(doubled * (1.0 - 0.5 * doubled) + 0.1)
    usable = (jnp.arange(TILE)[None, :] < counts[:, None]).reshape(-1).astype(jnp.float32)
    snp_count = new_dosage.shape[1]
    contract = (((1,), (1,)), ((), ()))
    local_rows = new_dosage.shape[0]
    usable_mine = lax.dynamic_slice_in_dim(usable, lax.axis_index(ROW) * local_rows, local_rows)
    scores_mine = ((new_dosage - doubled) / spread * usable_mine[:, None]).astype(jnp.bfloat16)
    new_scores = collect(scores_mine, ROW, 0)
    old_mine = ((old_dosage - doubled) / spread).astype(jnp.bfloat16)
    product = lax.dot_general(
        lax.all_gather(old_mine, COL, axis=0, tiled=True),
        new_scores,
        contract,
        preferred_element_type=jnp.float32,
    )
    row_count, col_count = product.shape
    scaled = (product / snp_count).reshape(row_count // TILE, TILE, col_count // TILE, TILE)
    masked_update = scaled * affected.astype(jnp.float32)[:, None, :, None]
    return (grm.astype(jnp.float32) + masked_update.reshape(row_count, col_count)).astype(
        jnp.bfloat16
    )


def solution(mesh):
    split = Mesh(mesh.devices.reshape(4, 4, 4, 2), ("row_0", "row_1", "col_0", "col_1"))
    placed = (P(COL_ROW, None), P(ROW_COL, None), P(ROW, COL), P(COL), P(ROW, COL))
    return jax.shard_map(
        on_device, mesh=split, in_specs=placed, out_specs=P(ROW, COL), check_vma=False
    )
```

profile of v0, /device:TPU:1, one launch (start us, length us, event | category | flops | bytes accessed | tf_op | source)
XLA Modules:
  0.0 100.6 jit_solution(6131358367804819225)
XLA Ops:
  6.5 0.0 all-gather.2.cloned.1.call-start
  6.5 1.3 %reduce_sum.9 = f32[1024]{0:T(1024)S(1)} reduce(f32[256,1024]{1,0:T(8,128)} %param.6, f32[]{:T(128)} %constant.12.clone.1), dimensions={0}, to_apply=%region_0.0 | reduce | flops 261120 | bytes 1052676 | tf_op jit(solution)/shard_map/reduce_sum | solution.py:40
  7.8 9.6 %psum.28 = f32[1024]{0:T(1024)S(1)} all-reduce(f32[1024]{0:T(1024)S(1)} %reduce_sum.9), channel_id=1, replica_groups=mesh['row_0'=4,'row_1'=4,'col_0'=4,'col_1'=2] {'row_0'}, use_global_device_ids=true, to_apply=%region_1.0 | all-reduce | flops 1024 | bytes 8192 | tf_op jit(solution)/shard_map/psum | solution.py:16
  17.4 9.7 %psum.29 = f32[1024]{0:T(1024)S(1)} all-reduce(f32[1024]{0:T(1024)S(1)} %psum.28), channel_id=1, replica_groups=mesh['row_0'=4,'row_1'=4,'col_0'=4,'col_1'=2] {'row_1'}, use_global_device_ids=true, to_apply=%region_2.0 | all-reduce | flops 1024 | bytes 8192 | tf_op jit(solution)/shard_map/psum | solution.py:16
  27.1 8.5 %psum.30 = f32[1024]{0:T(1024)S(1)} all-reduce(f32[1024]{0:T(1024)S(1)} %psum.29), channel_id=1, replica_groups=mesh['row_0'=4,'row_1'=4,'col_0'=4,'col_1'=2] {'col_0'}, use_global_device_ids=true, to_apply=%region_3.0 | all-reduce | flops 1024 | bytes 8192 | tf_op jit(solution)/shard_map/psum | solution.py:16
  35.6 8.9 %psum.31 = f32[1024]{0:T(1024)S(1)} all-reduce(f32[1024]{0:T(1024)S(1)} %psum.30), channel_id=1, replica_groups=mesh['row_0'=4,'row_1'=4,'col_0'=4,'col_1'=2] {'col_1'}, use_global_device_ids=true, to_apply=%region_4.0 | all-reduce | flops 1024 | bytes 8192 | tf_op jit(solution)/shard_map/psum | solution.py:16
  44.5 0.0 copy-start
  44.5 2.2 %divide_convert_fusion = bf16[256,1024]{1,0:T(8,128)(2,1)} fusion(f32[256,1024]{1,0:T(8,128)} %param.6, f32[1024]{0:T(1024)S(1)} %get-tuple-element.6, f32[1024]{0:T(1024)S(1)} %get-tuple-element.5), kind=kLoop, calls=%fused_computation.1 | loop fusion | flops 786432 | bytes 1581056 | tf_op jit(solution)/shard_map/convert_element_type | solution.py:50
  46.6 0.0 all-gather.2.cloned.1.call-update
  46.7 0.7 fusion
  47.4 0.1 dynamic_slice.3
  47.5 1.0 %multiply_convert_fusion = bf16[64,1024]{1,0:T(8,128)(2,1)S(1)} fusion(f32[64,1024]{1,0:T(8,128)} %param.5, f32[64]{0:T(128)S(1)} %dynamic_slice.3, f32[1024]{0:T(1024)S(1)} %get-tuple-element.6, f32[1024]{0:T(1024)S(1)} %get-tuple-element.5), kind=kLoop, calls=%fused_computation.2 | loop fusion | flops 262144 | bytes 401664 | tf_op jit(solution)/shard_map/convert_element_type | solution.py:48
  48.5 1.6 %broadcast_in_dim.2 = bf16[16,64,1024]{2,1,0:T(8,128)(2,1)} broadcast(bf16[64,1024]{1,0:T(8,128)(2,1)S(1)} %multiply_convert_fusion), dimensions={1,2} | broadcast | bytes 2228224 | tf_op jit(solution)/shard_map/broadcast_in_dim | solution.py:23
  50.1 3.7 %all-to-all-start = ((bf16[16,64,1024]{2,1,0:T(8,128)(2,1)}), bf16[16,64,1024]{2,1,0:T(8,128)(2,1)S(1)}, u32[]{:S(2)}, u32[]{:S(2)}) async-start(bf16[16,64,1024]{2,1,0:T(8,128)(2,1)} %broadcast_in_dim.2), calls=%async_computation | async-start | bytes 4194304 | tf_op jit(solution)/shard_map/all_to_all | solution.py:22
  53.9 0.0 copy-done
  53.9 0.1 copy.6
  54.0 5.4 %mul.41 = f32[4,512,2,512]{3,2,1,0:T(2,128)} broadcast(f32[4,2]{1,0:T(4,128)S(1)} %copy.6), dimensions={0,2} | broadcast | bytes 8388640 | tf_op jit(solution)/shard_map/mul | solution.py:59
  59.4 8.8 %copy.8 = f32[256,8,2,512]{3,1,2,0:T(8,128)} copy(f32[256,8,2,512]{3,2,1,0:T(2,128)} %bitcast.9) | data formatting | bytes 16777216
  68.2 14.8 %all-to-all-done = bf16[16,64,1024]{2,1,0:T(8,128)(2,1)S(1)} async-done(((bf16[16,64,1024]{2,1,0:T(8,128)(2,1)}), bf16[16,64,1024]{2,1,0:T(8,128)(2,1)S(1)}, u32[]{:S(2)}, u32[]{:S(2)}) %all-to-all-start) | async-done | bytes 2097184 | tf_op jit(solution)/shard_map/all_to_all | solution.py:22
  83.0 0.0 all-gather.2.cloned.1.call-done
  83.0 10.8 %add_convert_fusion = bf16[2048,1024]{1,0:T(8,128)(2,1)} fusion(f32[2048,1024]{1,0:T(8,128)} %bitcast.10, bf16[2048,1024]{1,0:T(8,128)(2,1)} %param.7, bf16[2048,1024]{1,0:T(8,128)(2,1)} %all-gather.2.cloned.1.call-done, bf16[1024,1024]{1,0:T(8,128)(2,1)S(1)} %bitcast.11), kind=kOutput, calls=%fused_computation | convolution fusion | flops 4305453056 | bytes 23068672 | tf_op jit(solution)/shard_map/dot_general | solution.py:51
  (3 shorter events, 0.0 us)
Async XLA Ops:
  6.5 76.4 %all-gather.2.cloned.1.call-start = ((), (), s32[]{:S(2)}) async-start(), calls=%async_computation.1 | async-start | bytes 4718592 | tf_op jit(solution)/shard_map/all_gather | solution.py:52
  44.5 9.4 %copy-start = (s32[4,2]{0,1:T(2,128)S(1)}, s32[4,2]{0,1:T(2,128)}, u32[]{:S(2)}) copy-start(s32[4,2]{0,1:T(2,128)} %param.9) | copy-start | bytes 100
  50.1 32.9 %all-to-all-start = ((bf16[16,64,1024]{2,1,0:T(8,128)(2,1)}), bf16[16,64,1024]{2,1,0:T(8,128)(2,1)S(1)}, u32[]{:S(2)}, u32[]{:S(2)}) async-start(bf16[16,64,1024]{2,1,0:T(8,128)(2,1)} %broadcast_in_dim.2), calls=%async_computation | async-start | bytes 4194304 | tf_op jit(solution)/shard_map/all_to_all | solution.py:22
Sparse Core Ops, SparseCore 0:
  46.8 26.7 all-gather.1
where the time goes:
time: 101 us
  blocking collectives  36.6 us (36%)
  local copies, waits for them, and re-layouts  16 us (16%)
  waiting for transfers between devices  14.8 us (15%)
  between operations  13.4 us (13%)
  matrix products  10.8 us (11%)
  other arithmetic  5.26 us (5%)
  starting transfers between devices  3.74 us (4%)
    psum x4, blocking collectives, one_axis_at_a_time(): shard = lax.psum(shard, axis)  36.6 us
    all_to_all x1, waiting for transfers between devices, sent_to_all(): lax.all_to_all(jnp.broadcast_to(shard[None], (length, *shard.shape)), axi...  14.8 us
    dot_general x1, matrix products, on_device(): lax.dot_general(lax.all_gather(old_mine, COL, axis=0, tiled=True), new_sc...  10.8 us
    unnamed x4, local copies, waits for them, and re-layouts  8.81 us
    mul x1, local copies, waits for them, and re-layouts, on_device(): masked_update = scaled * affected.astype(jnp.float32)[:, None, :, None]  5.44 us
    all_to_all x1, starting transfers between devices, sent_to_all(): lax.all_to_all(jnp.broadcast_to(shard[None], (length, *shard.shape)), axi...  3.73 us
    convert_element_type x1, other arithmetic, on_device(): old_mine = ((old_dosage - doubled) / spread).astype(jnp.bfloat16)  2.18 us
  transfers between devices with their start and end apart: 2, of which 1 were waited for; matrix products, arithmetic and copies ran while one was open for 18% of the time, Pallas kernels for 0%

commit v1 on v0

v1 whole, which is shorter than its diff:
```python
import functools

import jax
import jax.numpy as jnp
from jax import lax
from jax.experimental import pallas as pl
from jax.experimental.pallas import tpu as pltpu
from jax.sharding import PartitionSpec as P

MESH = pl.DeviceIdType.MESH
TILE = 512
SNP = 1024
RING = 4
CHUNKS = 4


def kernel(
    all_samples,
    old_hbm,
    new_hbm,
    grm_hbm,
    counts,
    affected,
    out,
    old_v,
    new_v,
    grm_v,
    a_v,
    b_v,
    mine1,
    mine2,
    s1,
    s2,
    load_sem,
    s1_send,
    s1_recv,
    s2_send,
    s2_recv,
    a_send,
    a_recv,
    b_send,
    b_recv,
):
    r = lax.axis_index("row")
    c = lax.axis_index("col")
    y, z = r // RING, r % RING
    x, core = c // 2, c % 2
    old_rows, new_rows = old_v.shape[0], new_v.shape[0]
    chunk = old_rows // CHUNKS
    unit = new_rows // 4

    load_old = pltpu.make_async_copy(old_hbm, old_v, load_sem.at[0])
    load_new = pltpu.make_async_copy(new_hbm, new_v, load_sem.at[1])
    load_grm = pltpu.make_async_copy(grm_hbm, grm_v, load_sem.at[2])
    load_old.start()
    load_new.start()
    barrier = pltpu.get_barrier_semaphore()
    for d in range(1, 8):
        pl.semaphore_signal(
            barrier, inc=1, device_id={"col": (c + d) % 8}, device_id_type=MESH
        )
    for d in range(1, 16):
        pl.semaphore_signal(
            barrier, inc=1, device_id={"row": (r + d) % 16}, device_id_type=MESH
        )
    load_grm.start()
    load_old.wait()
    mine1[...] = jnp.sum(old_v[...], axis=0, keepdims=True)
    pl.semaphore_wait(barrier, 22)

    def exchange(axis, me, size, mine, slots, send, recv):
        copies = []
        for d in range(1, size):
            copy = pltpu.make_async_remote_copy(
                src_ref=mine,
                dst_ref=slots.at[d],
                send_sem=send.at[d],
                recv_sem=recv.at[d],
                device_id={axis: (me + d) % size},
                device_id_type=MESH,
            )
            copy.start()
            copies.append(copy)
        total = mine[...]
        for d in range(1, size):
            copies[d - 1].wait_recv()
            total = total + slots[d]
        return total, copies

    total, copies1 = exchange("col", c, 8, mine1, s1, s1_send, s1_recv)
    mine2[...] = total
    total, copies2 = exchange("row", r, 16, mine2, s2, s2_send, s2_recv)
    doubled = total / all_samples
    inverse = 1.0 / jnp.sqrt(doubled * (1.0 - 0.5 * doubled) + 0.1)

    load_new.wait()
    position = (r % 8) * new_rows + lax.broadcasted_iota(jnp.int32, (new_rows, 1), 0)
    usable = (position < counts[0, r // 8]).astype(jnp.float32)
    b_v[pl.ds(pl.multiple_of(r * new_rows, new_rows), new_rows), :] = (
        (new_v[...] - doubled) * inverse * usable
    ).astype(jnp.bfloat16)

    sent = list(copies1) + list(copies2)
    b_index, a_index = {}, {}

    def send_to(ref, sends, recvs, index, key, device):
        slot = index.setdefault(key, len(index))
        copy = pltpu.make_async_remote_copy(
            src_ref=ref,
            dst_ref=ref,
            send_sem=sends.at[slot],
            recv_sem=recvs.at[slot],
            device_id=device,
            device_id_type=MESH,
        )
        copy.start()
        sent.append(copy)

    def arrived(ref, sends, recvs, index, key):
        slot = index.setdefault(key, len(index))
        pltpu.make_async_remote_copy(
            src_ref=ref,
            dst_ref=ref,
            send_sem=sends.at[slot],
            recv_sem=recvs.at[slot],
            device_id={"col": c},
            device_id_type=MESH,
        ).wait_recv()

    def b_block(h, df, ds, first, count):
        dy, dz = (ds, df) if h == 0 else (df, ds)
        block = ((y + dy + RING) % RING) * RING + (z + dz + RING) % RING
        start = block * new_rows + (2 * h + first) * unit
        return b_v.at[pl.ds(pl.multiple_of(start, unit), count * unit)]

    def b_device(h, stage, d):
        along_z = (h == 0) == (stage == 1)
        dy, dz = (0, d) if along_z else (d, 0)
        return {"row": ((y + dy + RING) % RING) * RING + (z + dz + RING) % RING}

    def b_send_block(h, stage, df, first=0, count=2, way=None, forward=False):
        for name, d in (("L", 1), ("R", -1)):
            if way in (None, name):
                key = (h, stage, 0 if stage == 1 else df, name + ("2" if forward else ""))
                if forward:
                    place = (-1 if name == "L" else 1)
                    ref = b_block(h, *((place, 0) if stage == 1 else (df, place)), first, count)
                else:
                    ref = b_block(h, *((0, 0) if stage == 1 else (df, 0)), first, count)
                send_to(ref, b_send, b_recv, b_index, key, b_device(h, stage, d))

    def b_arrived(h, stage, df, name):
        key = (h, stage, df, name)
        place = {"L": -1, "R": 1, "L2": -2, "R2": 2}[name]
        first, count = {"L": (0, 2), "R": (0, 2), "L2": (0, 1), "R2": (1, 1)}[name]
        ref = b_block(h, *((place, 0) if stage == 1 else (df, place)), first, count)
        arrived(ref, b_send, b_recv, b_index, key)

    def b_pass(h, stage, df, name):
        b_arrived(h, stage, df, name)
        b_send_block(h, stage, df, 0 if name == "L" else 1, 1, name, True)

    def a_block(dx, other):
        owner = ((x + dx + RING) % RING) * 2 + (1 - core if other else core)
        return owner

    def a_chunk(dx, other, i):
        start = a_block(dx, other) * old_rows + i * chunk
        return a_v.at[pl.ds(pl.multiple_of(start, chunk), chunk)]

    def a_to(ref, key, d):
        if d is None:
            device = {"col": x * 2 + 1 - core}
        else:
            device = {"col": ((x + d + RING) % RING) * 2 + core}
        send_to(ref, a_send, a_recv, a_index, key, device)

    def a_pass(name, i):
        dx = {"L": -1, "R": 1, "L2": -2, "R2": 2}[name]
        ref = a_chunk(dx, False, i)
        arrived(ref, a_send, a_recv, a_index, (name, i))
        if name == "L" and i < CHUNKS // 2:
            a_to(ref, ("L2", i), 1)
        if name == "R" and i >= CHUNKS // 2:
            a_to(ref, ("R2", i), -1)
        a_to(ref, ("P", abs(dx) if abs(dx) == 2 else dx, i), None)

    def a_from_partner(dx, i):
        arrived(a_chunk(dx, True, i), a_send, a_recv, a_index, ("P", dx, i))

    for h in (0, 1):
        b_send_block(h, 1, 0)
    half = CHUNKS // 2
    for i in range(CHUNKS):
        a_v[pl.ds(pl.multiple_of(c * old_rows + i * chunk, chunk), chunk), :] = (
            (old_v[pl.ds(i * chunk, chunk), :] - doubled) * inverse
        ).astype(jnp.bfloat16)
    for i in range(CHUNKS):
        a_to(a_chunk(0, False, i), ("L", i), 1)
        j = (i + half) % CHUNKS
        a_to(a_chunk(0, False, j), ("R", j), -1)
    for i in range(CHUNKS):
        a_to(a_chunk(0, False, i), ("P", 0, i), None)
    for h in (0, 1):
        b_send_block(h, 2, 0)
    for name in ("L", "R"):
        for h in (0, 1):
            b_pass(h, 1, 0, name)
    for df in (-1, 1):
        for h in (0, 1):
            b_send_block(h, 2, df)
    a_pass("L", 0)
    a_pass("R", half)
    for h in (0, 1):
        b_arrived(h, 1, 0, "L2")
        b_arrived(h, 1, 0, "R2")
        b_send_block(h, 2, 2)
    for name in ("L", "R"):
        for h in (0, 1):
            b_pass(h, 2, 0, name)
    a_pass("L", 1)
    a_pass("R", half + 1)
    for df in (-1, 1):
        for name in ("L", "R"):
            for h in (0, 1):
                b_pass(h, 2, df, name)
    a_pass("L", 2)
    a_pass("R", 0)
    for name in ("L", "R"):
        for h in (0, 1):
            b_pass(h, 2, 2, name)
    a_pass("L", 3)
    a_pass("R", 1)
    for df in (0, -1, 1, 2):
        for name in ("L2", "R2"):
            for h in (0, 1):
                b_arrived(h, 2, df, name)
    load_grm.wait()

    def update(owner):
        rows = pl.ds(pl.multiple_of(owner * old_rows, old_rows), old_rows)
        for j in range(2):
            columns = pl.ds(j * TILE, TILE)
            product = lax.dot_general(
                a_v[rows, :],
                b_v[columns, :],
                (((1,), (1,)), ((), ())),
                preferred_element_type=jnp.float32,
            )
            scale = affected[owner * old_rows // TILE, j].astype(jnp.float32) * (1.0 / SNP)
            out[rows, columns] = (
                grm_v[rows, columns].astype(jnp.float32) + product * scale
            ).astype(jnp.bfloat16)

    update(a_block(0, False))
    for i in range(CHUNKS):
        a_from_partner(0, i)
    update(a_block(0, True))
    update(a_block(-1, False))
    a_pass("L2", 0)
    a_pass("R2", half)
    for i in range(CHUNKS):
        a_from_partner(-1, i)
    update(a_block(-1, True))
    update(a_block(1, False))
    for i in range(CHUNKS):
        a_from_partner(1, i)
    update(a_block(1, True))
    a_pass("L2", 1)
    a_pass("R2", half + 1)
    update(a_block(2, False))
    for i in range(CHUNKS):
        a_from_partner(2, i)
    update(a_block(2, True))
    for copy in sent:
        copy.wait_send()


def on_device(new_dosage, old_dosage, grm, counts, affected):
    old_rows, snps = old_dosage.shape
    new_rows = new_dosage.shape[0]
    devices = lax.axis_size("row") * lax.axis_size("col")
    vmem, dma = pltpu.VMEM, pltpu.SemaphoreType.DMA
    hbm = pl.BlockSpec(memory_space=pltpu.HBM)
    smem = pl.BlockSpec(memory_space=pltpu.SMEM)
    return pl.pallas_call(
        functools.partial(kernel, float(old_rows * devices)),
        out_shape=jax.ShapeDtypeStruct(grm.shape, grm.dtype),
        in_specs=[hbm, hbm, hbm, smem, smem],
        out_specs=pl.BlockSpec(memory_space=pltpu.VMEM),
        scratch_shapes=[
            vmem((old_rows, snps), jnp.float32),
            vmem((new_rows, snps), jnp.float32),
            vmem(grm.shape, grm.dtype),
            vmem((grm.shape[0], snps), jnp.bfloat16),
            vmem((grm.shape[1], snps), jnp.bfloat16),
            vmem((1, snps), jnp.float32),
            vmem((1, snps), jnp.float32),
            vmem((8, 1, snps), jnp.float32),
            vmem((16, 1, snps), jnp.float32),
            dma((3,)),
            dma((8,)),
            dma((8,)),
            dma((16,)),
            dma((16,)),
            dma((28,)),
            dma((28,)),
            dma((40,)),
            dma((40,)),
        ],
        compiler_params=pltpu.CompilerParams(
            collective_id=0, has_side_effects=True, vmem_limit_bytes=40 * 1024 * 1024
        ),
    )(old_dosage, new_dosage, grm, counts.reshape(1, -1), affected)


def solution(mesh):
    placed = (
        P(("col", "row"), None),
        P(("row", "col"), None),
        P("row", "col"),
        P("col"),
        P("row", "col"),
    )
    return jax.shard_map(
        on_device, mesh=mesh, in_specs=placed, out_specs=P("row", "col"), check_vma=False
    )
```

time: 101 us -> 49.7 us (0.49)
  Pallas kernels: 0 us -> 41.7 us
  blocking collectives: 36.6 us -> 0 us
  waiting for transfers between devices: 14.8 us -> 0 us
  between operations: 13.4 us -> 0.01 us
  matrix products: 10.8 us -> 0 us
  local copies, waits for them, and re-layouts: 16 us -> 7.8 us
  other arithmetic: 5.26 us -> 0 us
  starting transfers between devices: 3.74 us -> 0 us
    pallas_call x0 -> x1, Pallas kernels: none -> 41.7 us  [on_device(): pl.pallas_call(functools.partial(kernel, float(old_rows * devices)), out_...]
    psum x4 -> x0, blocking collectives: 36.6 us -> none  [one_axis_at_a_time(): shard = lax.psum(shard, axis)]
    all_to_all x1 -> x0, waiting for transfers between devices: 14.8 us -> none  [sent_to_all(): lax.all_to_all(jnp.broadcast_to(shard[None], (length, *shard.shape)), axi...]
    dot_general x1 -> x0, matrix products: 10.8 us -> none  [on_device(): lax.dot_general(lax.all_gather(old_mine, COL, axis=0, tiled=True), new_sc...]
    mul x1 -> x0, local copies, waits for them, and re-layouts: 5.44 us -> none  [on_device(): masked_update = scaled * affected.astype(jnp.float32)[:, None, :, None]]
    all_to_all x1 -> x0, starting transfers between devices: 3.73 us -> none  [sent_to_all(): lax.all_to_all(jnp.broadcast_to(shard[None], (length, *shard.shape)), axi...]
    convert_element_type x3 -> x0, other arithmetic: 3.22 us -> none  [the longest x1 2.18 us: on_device(): old_mine = ((old_dosage - doubled) / spread).astype(jnp.bfloat16)]
    broadcast_in_dim x1 -> x0, local copies, waits for them, and re-layouts: 1.58 us -> none  [sent_to_all(): jnp.broadcast_to(shard[None], (length, *shard.shape))]
  transfers between devices with their start and end apart: 2 -> 0, of which waited for: 1 -> 0; matrix products, arithmetic and copies ran while one was open for 18% -> 0% of each run, Pallas kernels for 0% -> 0%
where the time goes in v1:
time: 49.7 us; the launch traced here: 49.5 us
  Pallas kernels  41.7 us (84%)
  local copies, waits for them, and re-layouts  7.8 us (16%)
    pallas_call x1, Pallas kernels, on_device(): pl.pallas_call(functools.partial(kernel, float(old_rows * devices)), out_...  41.7 us
    unnamed x10, local copies, waits for them, and re-layouts  7.8 us

profile of v1, /device:TPU:1, one launch (start us, length us, event | category | flops | bytes accessed | tf_op | source)
XLA Modules:
  0.0 49.5 jit_solution(15253541631600155886)
XLA Ops:
  0.0 0.8 %copy.6.affected = s32[4,2]{1,0:T(4,128)S(1)} copy(s32[4,2]{0,1:T(2,128)} %param.9) | data formatting | bytes 64 | tf_op args[4]
  0.8 0.0 copy-start
  0.8 2.2 %copy-done = bf16[2048,1024]{1,0:T(8,128)(2,1)S(1)} copy-done((bf16[2048,1024]{1,0:T(8,128)(2,1)S(1)}, bf16[2048,1024]{1,0:T(8,128)(2,1)}, u32[]{:S(2)}) %copy-start) | copy-done | bytes 4194328
  3.0 0.0 copy-start.1
  3.0 1.2 %copy-done.1 = f32[256,1024]{1,0:T(8,128)S(1)} copy-done((f32[256,1024]{1,0:T(8,128)S(1)}, f32[256,1024]{1,0:T(8,128)}, u32[]{:S(2)}) %copy-start.1) | copy-done | bytes 1048600
  4.2 0.0 copy-start.2
  4.2 0.9 %copy-done.2 = f32[64,1024]{1,0:T(8,128)S(1)} copy-done((f32[64,1024]{1,0:T(8,128)S(1)}, f32[64,1024]{1,0:T(8,128)}, u32[]{:S(2)}) %copy-start.2) | copy-done | bytes 262168
  5.1 0.0 copy-start.3
  5.1 0.7 %copy-done.3 = s32[2]{0:T(128)S(1)} copy-done((s32[2]{0:T(128)S(1)}, s32[2]{0:T(128)}, u32[]{:S(2)}) %copy-start.3) | copy-done | bytes 32
  5.8 41.7 %shard_map.55 = bf16[2048,1024]{1,0:T(8,128)(2,1)S(1)} custom-call(f32[256,1024]{1,0:T(8,128)S(1)} %copy-done.1, f32[64,1024]{1,0:T(8,128)S(1)} %copy-done.2, bf16[2048,1024]{1,0:T(8,128)(2,1)S(1)} %copy-done, s32[1,2]{1,0:T(1,128)S(1)} %bitcast.1, s32[4,2]{1,0:T(4,128)S(1)} %copy.6.affected), custom_call_target="tpu_custom_call" | custom-call | tf_op jit(solution)/shard_map/pallas_call | solution.py:286
  47.5 2.0 %copy.8 = bf16[2048,1024]{1,0:T(8,128)(2,1)} copy(bf16[2048,1024]{1,0:T(8,128)(2,1)S(1)} %shard_map.55) | data formatting | bytes 8388608
Async XLA Ops:
  0.8 2.2 %copy-start = (bf16[2048,1024]{1,0:T(8,128)(2,1)S(1)}, bf16[2048,1024]{1,0:T(8,128)(2,1)}, u32[]{:S(2)}) copy-start(bf16[2048,1024]{1,0:T(8,128)(2,1)} %grm_hbm.1) | copy-start | bytes 12582916
  3.0 1.2 %copy-start.1 = (f32[256,1024]{1,0:T(8,128)S(1)}, f32[256,1024]{1,0:T(8,128)}, u32[]{:S(2)}) copy-start(f32[256,1024]{1,0:T(8,128)} %old_hbm.1) | copy-start | bytes 3145732
  4.2 0.9 %copy-start.2 = (f32[64,1024]{1,0:T(8,128)S(1)}, f32[64,1024]{1,0:T(8,128)}, u32[]{:S(2)}) copy-start(f32[64,1024]{1,0:T(8,128)} %new_hbm.1) | copy-start | bytes 786436
  5.1 0.7 %copy-start.3 = (s32[2]{0:T(128)S(1)}, s32[2]{0:T(128)}, u32[]{:S(2)}) copy-start(s32[2]{0:T(128)} %param.8) | copy-start | bytes 28

commit v2 on v1

--- a/solution.py
+++ b/solution.py
@@ -19,9 +19,11 @@
     old_hbm,
     new_hbm,
     grm_hbm,
+    counts_hbm,
+    affected_hbm,
+    out,
     counts,
     affected,
-    out,
     old_v,
     new_v,
     grm_v,
@@ -54,6 +56,10 @@
     load_grm = pltpu.make_async_copy(grm_hbm, grm_v, load_sem.at[2])
     load_old.start()
     load_new.start()
+    load_counts = pltpu.make_async_copy(counts_hbm, counts, load_sem.at[3])
+    load_affected = pltpu.make_async_copy(affected_hbm, affected, load_sem.at[4])
+    load_counts.start()
+    load_affected.start()
     barrier = pltpu.get_barrier_semaphore()
     for d in range(1, 8):
         pl.semaphore_signal(
@@ -94,6 +100,8 @@
     inverse = 1.0 / jnp.sqrt(doubled * (1.0 - 0.5 * doubled) + 0.1)
 
     load_new.wait()
+    load_counts.wait()
+    load_affected.wait()
     position = (r % 8) * new_rows + lax.broadcasted_iota(jnp.int32, (new_rows, 1), 0)
     usable = (position < counts[0, r // 8]).astype(jnp.float32)
     b_v[pl.ds(pl.multiple_of(r * new_rows, new_rows), new_rows), :] = (
@@ -247,7 +255,7 @@
                 (((1,), (1,)), ((), ())),
                 preferred_element_type=jnp.float32,
             )
-            scale = affected[owner * old_rows // TILE, j].astype(jnp.float32) * (1.0 / SNP)
+            scale = affected[j, owner * old_rows // TILE].astype(jnp.float32) * (1.0 / SNP)
             out[rows, columns] = (
                 grm_v[rows, columns].astype(jnp.float32) + product * scale
             ).astype(jnp.bfloat16)
@@ -282,13 +290,15 @@
     devices = lax.axis_size("row") * lax.axis_size("col")
     vmem, dma = pltpu.VMEM, pltpu.SemaphoreType.DMA
     hbm = pl.BlockSpec(memory_space=pltpu.HBM)
-    smem = pl.BlockSpec(memory_space=pltpu.SMEM)
+    operands = (old_dosage, new_dosage, grm, counts.reshape(1, -1), affected.T)
     return pl.pallas_call(
         functools.partial(kernel, float(old_rows * devices)),
         out_shape=jax.ShapeDtypeStruct(grm.shape, grm.dtype),
-        in_specs=[hbm, hbm, hbm, smem, smem],
+        in_specs=[hbm] * len(operands),
         out_specs=pl.BlockSpec(memory_space=pltpu.VMEM),
         scratch_shapes=[
+            pltpu.SMEM((1, counts.shape[0]), jnp.int32),
+            pltpu.SMEM(affected.shape[::-1], jnp.int32),
             vmem((old_rows, snps), jnp.float32),
             vmem((new_rows, snps), jnp.float32),
             vmem(grm.shape, grm.dtype),
@@ -298,7 +308,7 @@
             vmem((1, snps), jnp.float32),
             vmem((8, 1, snps), jnp.float32),
             vmem((16, 1, snps), jnp.float32),
-            dma((3,)),
+            dma((5,)),
             dma((8,)),
             dma((8,)),
             dma((16,)),
@@ -311,7 +321,7 @@
         compiler_params=pltpu.CompilerParams(
             collective_id=0, has_side_effects=True, vmem_limit_bytes=40 * 1024 * 1024
         ),
-    )(old_dosage, new_dosage, grm, counts.reshape(1, -1), affected)
+    )(*[pltpu.with_memory_space_constraint(operand, pltpu.HBM) for operand in operands])
 
 
 def solution(mesh):

time: 49.7 us -> 43.1 us (0.87)
  local copies, waits for them, and re-layouts: 7.8 us -> 2.02 us
  Pallas kernels: 41.7 us -> 41 us
    unnamed x10 -> x1, local copies, waits for them, and re-layouts: 7.8 us -> 2.02 us
    pallas_call x1, Pallas kernels: 41.7 us -> 41 us  [on_device(): pl.pallas_call(functools.partial(kernel, float(old_rows * devices)), out_...]
where the time goes in v2:
time: 43.1 us; the launch traced here: 43 us
  Pallas kernels  41 us (95%)
  local copies, waits for them, and re-layouts  2.02 us (5%)
    pallas_call x1, Pallas kernels, on_device(): pl.pallas_call(functools.partial(kernel, float(old_rows * devices)), out_...  41 us
    unnamed x1, local copies, waits for them, and re-layouts  2.02 us

profile of v2, /device:TPU:1, one launch (start us, length us, event | category | flops | bytes accessed | tf_op | source)
XLA Modules:
  0.0 43.0 jit_solution(7376953819384469190)
XLA Ops:
  0.0 41.0 %shard_map.55 = bf16[2048,1024]{1,0:T(8,128)(2,1)S(1)} custom-call(f32[256,1024]{1,0:T(8,128)} %old_hbm.1, f32[64,1024]{1,0:T(8,128)} %new_hbm.1, bf16[2048,1024]{1,0:T(8,128)(2,1)} %grm_hbm.1, s32[1,2]{1,0:T(1,128)} %bitcast.3, s32[2,4]{1,0:T(2,128)} %bitcast.2), custom_call_target="tpu_custom_call" | custom-call | tf_op jit(solution)/shard_map/pallas_call | solution.py:294
  41.0 2.0 %copy.7 = bf16[2048,1024]{1,0:T(8,128)(2,1)} copy(bf16[2048,1024]{1,0:T(8,128)(2,1)S(1)} %shard_map.55) | data formatting | bytes 8388608

commit v3 on v0

v3 whole, which is shorter than its diff:
```python
import functools

import jax
import jax.numpy as jnp
from jax import lax
from jax.experimental import pallas as pl
from jax.experimental.pallas import tpu as pltpu
from jax.sharding import PartitionSpec as P

MESH = pl.DeviceIdType.MESH
TILE = 512
SNP = 1024
RING = 4
RAW = 64
CHUNKS = 4
COPIES = 54 + 6 * CHUNKS
PLACE = {"L": -1, "R": 1, "L2": 2, "R2": 2}


def contract(left, right):
    return lax.dot_general(
        left, right, (((1,), (1,)), ((), ())), preferred_element_type=jnp.float32
    )


def gather_kernel(
    all_samples,
    old_hbm,
    new_hbm,
    grm_hbm,
    counts_hbm,
    affected_hbm,
    out,
    b_v,
    a_last,
    scale_last,
    counts,
    affected,
    old_v,
    new_v,
    a_v,
    a_raw,
    b_raw,
    mine1,
    mine2,
    s1,
    s2,
    load_sem,
    s1_send,
    s1_recv,
    s2_send,
    s2_recv,
    send_sem,
    recv_sem,
):
    r = lax.axis_index("row")
    c = lax.axis_index("col")
    y, z = r // RING, r % RING
    x, core = c // 2, c % 2
    old_rows, new_rows = old_v.shape[0], new_v.shape[0]
    chunk = (old_rows - RAW) // CHUNKS
    unit = new_rows // 4
    sent, index = [], {}

    def at_col(dx, flip=False):
        return {"col": ((x + dx + RING) % RING) * 2 + (1 - core if flip else core)}

    def at_row(dy, dz):
        return {"row": ((y + dy + RING) % RING) * RING + (z + dz + RING) % RING}

    def copy_of(source, target, key, device):
        slot = index.setdefault(key, len(index))
        return pltpu.make_async_remote_copy(
            src_ref=source,
            dst_ref=target,
            send_sem=send_sem.at[slot],
            recv_sem=recv_sem.at[slot],
            device_id=device,
            device_id_type=MESH,
        )

    def send(source, target, key, device):
        copy = copy_of(source, target, key, device)
        copy.start()
        sent.append(copy)

    def arrived(target, key):
        copy_of(target, target, key, {"col": c}).wait_recv()

    def rows_of(ref, start, count, step):
        return ref.at[pl.ds(pl.multiple_of(start, step), count)]

    load_old = pltpu.make_async_copy(old_hbm, old_v, load_sem.at[0])
    load_new = pltpu.make_async_copy(new_hbm, new_v, load_sem.at[1])
    load_grm = pltpu.make_async_copy(grm_hbm, out, load_sem.at[2])
    load_counts = pltpu.make_async_copy(counts_hbm, counts, load_sem.at[3])
    load_affected = pltpu.make_async_copy(affected_hbm, affected, load_sem.at[4])
    load_old.start()
    load_new.start()
    load_counts.start()
    load_affected.start()
    barrier = pltpu.get_barrier_semaphore()
    for d in range(1, 8):
        pl.semaphore_signal(
            barrier, inc=1, device_id={"col": (c + d) % 8}, device_id_type=MESH
        )
    for d in range(1, 16):
        pl.semaphore_signal(
            barrier, inc=1, device_id={"row": (r + d) % 16}, device_id_type=MESH
        )
    load_grm.start()
    load_old.wait()
    mine1[...] = jnp.sum(old_v[...], axis=0, keepdims=True)
    load_new.wait()
    pl.semaphore_wait(barrier, 22)

    def exchange(axis, me, size, mine, slots, sends, recvs):
        copies = []
        for d in range(1, size):
            copy = pltpu.make_async_remote_copy(
                src_ref=mine,
                dst_ref=slots.at[d],
                send_sem=sends.at[d],
                recv_sem=recvs.at[d],
                device_id={axis: (me + d) % size},
                device_id_type=MESH,
            )
            copy.start()
            copies.append(copy)
            sent.append(copy)
        return copies

    def added(mine, slots, copies):
        total = mine[...]
        for d, copy in enumerate(copies, 1):
            copy.wait_recv()
            total = total + slots[d]
        return total

    def raw_half(owner, i):
        return a_raw.at[owner, pl.ds(i * (RAW // 2), RAW // 2)]

    def raw_owner(dx, flip=False):
        return at_col(dx, flip)["col"]

    copies1 = exchange("col", c, 8, mine1, s1, s1_send, s1_recv)
    for h in (0, 1):
        source = new_v.at[pl.ds(h * 2 * unit, 2 * unit)]
        for name, d in (("L", 1), ("R", -1)):
            device = at_row(0, d) if h == 0 else at_row(d, 0)
            send(source, b_raw.at[3 * h + (d < 0)], ("b1", h, name), device)
    for i in (0, 1):
        for name, d, j in (("L", 1, i), ("R", -1, 1 - i)):
            source = old_v.at[pl.ds(j * (RAW // 2), RAW // 2)]
            send(source, raw_half(c, j), ("raw", name, j), at_col(d))
    send(old_v.at[pl.ds(0, RAW)], a_raw.at[c], ("rawP", 0), at_col(0, True))
    mine2[...] = added(mine1, s1, copies1)
    copies2 = exchange("row", r, 16, mine2, s2, s2_send, s2_recv)
    for name, d, u in (("L", 1, 0), ("R", -1, 1)):
        for h in (0, 1):
            source = b_raw.at[3 * h + (d < 0)]
            arrived(source, ("b1", h, name))
            device = at_row(0, d) if h == 0 else at_row(d, 0)
            part = pl.ds(u * unit, unit)
            send(source.at[part], b_raw.at[3 * h + 2, part], ("b1", h, name + "2"), device)

    def raw_pass(name, i):
        owner = raw_owner(PLACE[name])
        source = raw_half(owner, i)
        arrived(source, ("raw", name, i))
        if (name, i) == ("L", 0):
            send(source, source, ("raw", "L2", i), at_col(1))
        if (name, i) == ("R", 1):
            send(source, source, ("raw", "R2", i), at_col(-1))
        send(source, source, ("rawP", PLACE[name], i), at_col(0, True))

    raw_pass("L", 0)
    raw_pass("R", 1)
    total = added(mine2, s2, copies2)
    doubled = total / all_samples
    inverse = 1.0 / jnp.sqrt(doubled * (1.0 - 0.5 * doubled) + 0.1)

    def scored(dosage):
        return (dosage - doubled) * inverse

    def a_rows(dx, flip, start, count):
        if dx == 2:
            half = (1 - core if flip else core) * old_rows
            return rows_of(a_last, half + start, count, 16)
        return rows_of(a_v, raw_owner(dx, flip) * old_rows + start, count, 16)

    def a_chunk(dx, flip, i):
        return a_rows(dx, flip, RAW + i * chunk, chunk)

    mine = raw_owner(0)

    def a_send_own(name, d, i):
        chunk_of = a_chunk(0, False, i)
        send(chunk_of, chunk_of, ("a", name, i), at_col(d))

    half = CHUNKS // 2
    for i in range(half):
        for j in (i, i + half):
            a_chunk(0, False, j)[...] = scored(
                old_v[pl.ds(RAW + j * chunk, chunk), :]
            ).astype(jnp.bfloat16)
        a_send_own("L", 1, i)
        a_send_own("R", -1, i + half)
    for i in range(half):
        a_send_own("L", 1, i + half)
        a_send_own("R", -1, i)
    a_rows(0, False, 0, RAW)[...] = scored(old_v[pl.ds(0, RAW), :]).astype(jnp.bfloat16)

    def b_row(h, df, ds):
        dy, dz = (ds, df) if h == 0 else (df, ds)
        return at_row(dy, dz)["row"]

    def b_part(h, df, ds, first=0, count=2):
        start = b_row(h, df, ds) * new_rows + (2 * h + first) * unit
        return rows_of(b_v, start, count * unit, unit)

    load_counts.wait()

    def b_score(h, df, source):
        row = b_row(h, df, 0)
        first = (row % 8) * new_rows + 2 * h * unit
        position = first + lax.broadcasted_iota(jnp.int32, (2 * unit, 1), 0)
        usable = (position < counts[0, row // 8]).astype(jnp.float32)
        b_part(h, df, 0)[...] = (scored(source[...]) * usable).astype(jnp.bfloat16)
        for name, d in (("L", 1), ("R", -1)):
            device = at_row(d, 0) if h == 0 else at_row(0, d)
            send(b_part(h, df, 0), b_part(h, df, 0), ("b2", h, df, name), device)

    for h in (0, 1):
        b_score(h, 0, new_v.at[pl.ds(h * 2 * unit, 2 * unit)])
    for df in (-1, 1):
        for h in (0, 1):
            b_score(h, df, b_raw.at[3 * h + (df > 0)])
    for h in (0, 1):
        for name, u in (("L2", 0), ("R2", 1)):
            arrived(b_raw.at[3 * h + 2, pl.ds(u * unit, unit)], ("b1", h, name))
        b_score(h, 2, b_raw.at[3 * h + 2])

    def b_pass(df):
        for name, d, u in (("L", 1, 0), ("R", -1, 1)):
            for h in (0, 1):
                arrived(b_part(h, df, PLACE[name]), ("b2", h, df, name))
                source = b_part(h, df, PLACE[name], u, 1)
                device = at_row(d, 0) if h == 0 else at_row(0, d)
                send(source, source, ("b2", h, df, name + "2"), device)

    def a_pass(name, i):
        dx = PLACE[name]
        source = a_chunk(dx, False, i)
        arrived(source, ("a", name, i))
        if name == "L" and i < half:
            send(source, rows_of(a_last, core * old_rows + RAW + i * chunk, chunk, 16), ("a", "L2", i), at_col(1))
        if name == "R" and i >= half:
            send(source, rows_of(a_last, core * old_rows + RAW + i * chunk, chunk, 16), ("a", "R2", i), at_col(-1))
        send(source, source, ("aP", dx, i), at_col(0, True))

    def raw_scored(dx, flip):
        a_rows(dx, flip, 0, RAW)[...] = scored(a_raw[raw_owner(dx, flip)]).astype(jnp.bfloat16)

    own_part = a_rows(0, False, RAW, old_rows - RAW)
    send(own_part, own_part, ("aP", 0), at_col(0, True))
    raw_pass("L", 1)
    raw_pass("R", 0)
    arrived(a_raw.at[raw_owner(0, True)], ("rawP", 0))
    raw_scored(0, True)
    raw_scored(-1, False)
    raw_scored(1, False)
    raw_pass("L2", 0)
    raw_pass("R2", 1)
    b_pass(0)
    a_pass("L", 0)
    a_pass("R", half)
    b_pass(-1)
    a_pass("L", 1)
    a_pass("R", half + 1)
    b_pass(1)
    raw_scored(2, False)
    for dx in (-1, 1, 2):
        for i in (0, 1):
            arrived(raw_half(raw_owner(dx, True), i), ("rawP", dx, i))
        raw_scored(dx, True)
    for i in range(half):
        a_pass("L", half + i)
        a_pass("R", i)
        if i == 0:
            b_pass(2)
    load_affected.wait()
    last_tile = (x + 2) % RING
    for j in range(2):
        scale_last[:, pl.ds(j * TILE, TILE)] = jnp.full(
            (8, TILE), affected[j, last_tile].astype(jnp.float32) * (1.0 / SNP)
        )
    for df in (0, -1, 1, 2):
        for name, u, place in (("L2", 0, -2), ("R2", 1, 2)):
            for h in (0, 1):
                arrived(b_part(h, df, place, u, 1), ("b2", h, df, name))
    load_grm.wait()

    def update(dx, flip):
        owner = raw_owner(dx, flip)
        rows = pl.ds(pl.multiple_of(owner * old_rows, old_rows), old_rows)
        for j in range(2):
            columns = pl.ds(j * TILE, TILE)
            product = contract(a_v[rows, :], b_v[columns, :])
            scale = affected[j, owner * old_rows // TILE].astype(jnp.float32) * (1.0 / SNP)
            out[rows, columns] = (
                out[rows, columns].astype(jnp.float32) + product * scale
            ).astype(jnp.bfloat16)

    update(0, False)
    own_other = a_rows(0, True, RAW, old_rows - RAW)
    arrived(own_other, ("aP", 0))
    update(0, True)
    update(-1, False)
    for i in range(half):
        if i < half - 1:
            a_pass("L2", i)
            a_pass("R2", half + i)
    update(1, False)
    for dx in (-1, 1):
        for i in range(CHUNKS):
            arrived(a_chunk(dx, True, i), ("aP", dx, i))
        update(dx, True)
    a_pass("L2", half - 1)
    a_pass("R2", CHUNKS - 1)
    for i in range(CHUNKS):
        arrived(a_chunk(2, True, i), ("aP", 2, i))
    for copy in sent:
        copy.wait_send()
    assert len(index) == COPIES, len(index)


def finish_kernel(updated, b_v, a_last, scale_last, result, last, store_sem):
    x = lax.axis_index("col") // 2
    rows = a_last.shape[0]
    stores = []

    def store(source, start, count, columns):
        start = pl.multiple_of(start, count)
        copy = pltpu.make_async_copy(
            source, result.at[pl.ds(start, count), columns], store_sem.at[len(stores)]
        )
        copy.start()
        stores.append(copy)

    whole = pl.ds(0, updated.shape[1])
    for d in (0, 1, 3):
        start = ((x + d) % RING) * rows
        store(updated.at[pl.ds(pl.multiple_of(start, rows), rows)], start, rows, whole)
    mine = ((x + 2) % RING) * rows
    piece = rows // 2
    for i in range(2):
        for j in range(2):
            columns = pl.ds(j * TILE, TILE)
            product = contract(a_last[pl.ds(i * piece, piece), :], b_v[columns, :])
            at = pl.ds(pl.multiple_of(mine + i * piece, piece), piece)
            last[pl.ds(i * piece, piece), columns] = (
                updated[at, columns].astype(jnp.float32) + product * scale_last[0:1, columns]
            ).astype(jnp.bfloat16)
            store(last.at[pl.ds(i * piece, piece), columns], mine + i * piece, piece, columns)
    for copy in stores:
        copy.wait()


def on_device(new_dosage, old_dosage, grm, counts, affected):
    old_rows, snps = old_dosage.shape
    new_rows = new_dosage.shape[0]
    devices = lax.axis_size("row") * lax.axis_size("col")
    vmem, dma = pltpu.VMEM, pltpu.SemaphoreType.DMA
    hbm_spec = pl.BlockSpec(memory_space=pltpu.HBM)
    vmem_spec = pl.BlockSpec(memory_space=pltpu.VMEM)
    operands = (old_dosage, new_dosage, grm, counts.reshape(1, -1), affected.T)
    parts = pl.pallas_call(
        functools.partial(gather_kernel, float(old_rows * devices)),
        out_shape=[
            pltpu.VMEM(grm.shape, grm.dtype),
            pltpu.VMEM((grm.shape[1], snps), jnp.bfloat16),
            pltpu.VMEM((2 * old_rows, snps), jnp.bfloat16),
            pltpu.VMEM((8, grm.shape[1]), jnp.float32),
        ],
        in_specs=[hbm_spec] * len(operands),
        out_specs=[vmem_spec] * 4,
        scratch_shapes=[
            pltpu.SMEM((1, counts.shape[0]), jnp.int32),
            pltpu.SMEM(affected.shape[::-1], jnp.int32),
            vmem((old_rows, snps), jnp.float32),
            vmem((new_rows, snps), jnp.float32),
            vmem((grm.shape[0], snps), jnp.bfloat16),
            vmem((8, RAW, snps), jnp.float32),
            vmem((6, new_rows // 2, snps), jnp.float32),
            vmem((1, snps), jnp.float32),
            vmem((1, snps), jnp.float32),
            vmem((8, 1, snps), jnp.float32),
            vmem((16, 1, snps), jnp.float32),
            dma((5,)),
            dma((8,)),
            dma((8,)),
            dma((16,)),
            dma((16,)),
            dma((COPIES,)),
            dma((COPIES,)),
        ],
        compiler_params=pltpu.CompilerParams(
            collective_id=0, has_side_effects=True, vmem_limit_bytes=40 * 1024 * 1024
        ),
        name="gather",
    )(*[pltpu.with_memory_space_constraint(operand, pltpu.HBM) for operand in operands])
    return pl.pallas_call(
        finish_kernel,
        out_shape=jax.ShapeDtypeStruct(grm.shape, grm.dtype),
        in_specs=[vmem_spec] * 4,
        out_specs=hbm_spec,
        scratch_shapes=[vmem((2 * old_rows, grm.shape[1]), grm.dtype), dma((7,))],
        compiler_params=pltpu.CompilerParams(vmem_limit_bytes=16 * 1024 * 1024),
        name="finish",
    )(*[pltpu.with_memory_space_constraint(part, pltpu.VMEM) for part in parts])


def solution(mesh):
    placed = (
        P(("col", "row"), None),
        P(("row", "col"), None),
        P("row", "col"),
        P("col"),
        P("row", "col"),
    )
    return jax.shard_map(
        on_device, mesh=mesh, in_specs=placed, out_specs=P("row", "col"), check_vma=False
    )
```

time: 101 us -> 40 us (0.40)
  Pallas kernels: 0 us -> 39.8 us
  blocking collectives: 36.6 us -> 0 us
  local copies, waits for them, and re-layouts: 16 us -> 0 us
  waiting for transfers between devices: 14.8 us -> 0 us
  between operations: 13.4 us -> 0.01 us
  matrix products: 10.8 us -> 0 us
  other arithmetic: 5.26 us -> 0 us
  starting transfers between devices: 3.74 us -> 0 us
    pallas_call x0 -> x2, Pallas kernels: none -> 39.8 us  [the longest x1 37.8 us: on_device(): pl.pallas_call(functools.partial(gather_kernel, float(old_rows * devices)...]
    psum x4 -> x0, blocking collectives: 36.6 us -> none  [one_axis_at_a_time(): shard = lax.psum(shard, axis)]
    all_to_all x1 -> x0, waiting for transfers between devices: 14.8 us -> none  [sent_to_all(): lax.all_to_all(jnp.broadcast_to(shard[None], (length, *shard.shape)), axi...]
    dot_general x1 -> x0, matrix products: 10.8 us -> none  [on_device(): lax.dot_general(lax.all_gather(old_mine, COL, axis=0, tiled=True), new_sc...]
    unnamed x4 -> x0, local copies, waits for them, and re-layouts: 8.81 us -> none
    mul x1 -> x0, local copies, waits for them, and re-layouts: 5.44 us -> none  [on_device(): masked_update = scaled * affected.astype(jnp.float32)[:, None, :, None]]
    all_to_all x1 -> x0, starting transfers between devices: 3.73 us -> none  [sent_to_all(): lax.all_to_all(jnp.broadcast_to(shard[None], (length, *shard.shape)), axi...]
    convert_element_type x3 -> x0, other arithmetic: 3.22 us -> none  [the longest x1 2.18 us: on_device(): old_mine = ((old_dosage - doubled) / spread).astype(jnp.bfloat16)]
  transfers between devices with their start and end apart: 2 -> 0, of which waited for: 1 -> 0; matrix products, arithmetic and copies ran while one was open for 18% -> 0% of each run, Pallas kernels for 0% -> 0%
where the time goes in v3:
time: 40 us; the launch traced here: 39.9 us
  Pallas kernels  39.8 us (99%)
    pallas_call x1, Pallas kernels, on_device(): pl.pallas_call(functools.partial(gather_kernel, float(old_rows * devices)...  37.8 us
    pallas_call x1, Pallas kernels, on_device(): pl.pallas_call(finish_kernel, out_shape=jax.ShapeDtypeStruct(grm.shape, g...  2.08 us

profile of v3, /device:TPU:1, one launch (start us, length us, event | category | flops | bytes accessed | tf_op | source)
XLA Modules:
  0.0 39.9 jit_solution(15008794090232526889)
XLA Ops:
  0.0 37.8 %gather.1 = (bf16[2048,1024]{1,0:T(8,128)(2,1)S(1)}, bf16[1024,1024]{1,0:T(8,128)(2,1)S(1)}, bf16[512,1024]{1,0:T(8,128)(2,1)S(1)}, f32[8,1024]{1,0:T(8,128)S(1)}) custom-call(f32[256,1024]{1,0:T(8,128)} %old_hbm.1, f32[64,1024]{1,0:T(8,128)} %new_hbm.1, bf16[2048,1024]{1,0:T(8,128)(2,1)} %grm_hbm.1, s32[1,2]{1,0:T(1,128)} %bitcast.3, s32[2,4]{1,0:T(2,128)} %bitcast.2), custom_call_target="tpu_custom_call" | custom-call | tf_op jit(solution)/shard_map/gather/pallas_call | solution.py:378
  37.8 2.1 %finish.1 = bf16[2048,1024]{1,0:T(8,128)(2,1)} custom-call(bf16[2048,1024]{1,0:T(8,128)(2,1)S(1)} %get-tuple-element.9.updated, bf16[1024,1024]{1,0:T(8,128)(2,1)S(1)} %get-tuple-element.10.b_v, bf16[512,1024]{1,0:T(8,128)(2,1)S(1)} %get-tuple-element.11.a_last, f32[8,1024]{1,0:T(8,128)S(1)} %get-tuple-element.12.scale_last), custom_call_target="tpu_custom_call" | custom-call | tf_op jit(solution)/shard_map/finish/pallas_call | solution.py:413

commit v4 on v3

--- a/solution.py
+++ b/solution.py
@@ -1,4 +1,5 @@
 import functools
+import math
 
 import jax
 import jax.numpy as jnp
@@ -13,7 +14,7 @@
 RING = 4
 RAW = 64
 CHUNKS = 4
-COPIES = 54 + 6 * CHUNKS
+ARRIVALS = 24 + 3 * CHUNKS
 PLACE = {"L": -1, "R": 1, "L2": 2, "R2": 2}
 
 
@@ -46,10 +47,6 @@
     s1,
     s2,
     load_sem,
-    s1_send,
-    s1_recv,
-    s2_send,
-    s2_recv,
     send_sem,
     recv_sem,
 ):
@@ -60,7 +57,7 @@
     old_rows, new_rows = old_v.shape[0], new_v.shape[0]
     chunk = (old_rows - RAW) // CHUNKS
     unit = new_rows // 4
-    sent, index = [], {}
+    index, sent_rows = {}, {}
 
     def at_col(dx, flip=False):
         return {"col": ((x + dx + RING) % RING) * 2 + (1 - core if flip else core)}
@@ -68,24 +65,25 @@
     def at_row(dy, dz):
         return {"row": ((y + dy + RING) % RING) * RING + (z + dz + RING) % RING}
 
-    def copy_of(source, target, key, device):
-        slot = index.setdefault(key, len(index))
+    def copy_of(source, target, key, group, device):
         return pltpu.make_async_remote_copy(
             src_ref=source,
             dst_ref=target,
-            send_sem=send_sem.at[slot],
-            recv_sem=recv_sem.at[slot],
+            send_sem=send_sem.at[group],
+            recv_sem=recv_sem.at[index.setdefault(key, len(index))],
             device_id=device,
             device_id_type=MESH,
         )
 
     def send(source, target, key, device):
-        copy = copy_of(source, target, key, device)
-        copy.start()
-        sent.append(copy)
-
-    def arrived(target, key):
-        copy_of(target, target, key, {"col": c}).wait_recv()
+        group = {"raw": 0, "rawP": 0, "b1": 0, "b2": 1, "a": 2, "aP": 2}[key[0]]
+        copy_of(source, target, key, group, device).start()
+        rows = math.prod(source.shape) * source.dtype.itemsize // (2 * SNP)
+        sent_rows[group] = sent_rows.get(group, 0) + rows
+
+    def arrived(key, rows):
+        target = out.at[pl.ds(0, rows)]
+        copy_of(target, target, key, 0, {"col": c}).wait_recv()
 
     def rows_of(ref, start, count, step):
         return ref.at[pl.ds(pl.multiple_of(start, step), count)]
@@ -114,26 +112,15 @@
     load_new.wait()
     pl.semaphore_wait(barrier, 22)
 
-    def exchange(axis, me, size, mine, slots, sends, recvs):
-        copies = []
+    def exchange(axis, me, size, mine, slots, group):
         for d in range(1, size):
-            copy = pltpu.make_async_remote_copy(
-                src_ref=mine,
-                dst_ref=slots.at[d],
-                send_sem=sends.at[d],
-                recv_sem=recvs.at[d],
-                device_id={axis: (me + d) % size},
-                device_id_type=MESH,
-            )
-            copy.start()
-            copies.append(copy)
-            sent.append(copy)
-        return copies
-
-    def added(mine, slots, copies):
+            copy_of(mine, slots.at[d], axis, group, {axis: (me + d) % size}).start()
+
+    def exchanged(axis, size, mine, slots, group):
+        landed = slots.at[pl.ds(1, size - 1)]
+        copy_of(landed, landed, axis, group, {"col": c}).wait_recv()
         total = mine[...]
-        for d, copy in enumerate(copies, 1):
-            copy.wait_recv()
+        for d in range(1, size):
             total = total + slots[d]
         return total
 
@@ -143,40 +130,40 @@
     def raw_owner(dx, flip=False):
         return at_col(dx, flip)["col"]
 
-    copies1 = exchange("col", c, 8, mine1, s1, s1_send, s1_recv)
+    exchange("col", c, 8, mine1, s1, 3)
     for h in (0, 1):
         source = new_v.at[pl.ds(h * 2 * unit, 2 * unit)]
         for name, d in (("L", 1), ("R", -1)):
             device = at_row(0, d) if h == 0 else at_row(d, 0)
-            send(source, b_raw.at[3 * h + (d < 0)], ("b1", h, name), device)
+            send(source, b_raw.at[3 * h + (d < 0)], ("b1", name), device)
     for i in (0, 1):
         for name, d, j in (("L", 1, i), ("R", -1, 1 - i)):
             source = old_v.at[pl.ds(j * (RAW // 2), RAW // 2)]
             send(source, raw_half(c, j), ("raw", name, j), at_col(d))
     send(old_v.at[pl.ds(0, RAW)], a_raw.at[c], ("rawP", 0), at_col(0, True))
-    mine2[...] = added(mine1, s1, copies1)
-    copies2 = exchange("row", r, 16, mine2, s2, s2_send, s2_recv)
+    mine2[...] = exchanged("col", 8, mine1, s1, 3)
+    exchange("row", r, 16, mine2, s2, 4)
     for name, d, u in (("L", 1, 0), ("R", -1, 1)):
+        arrived(("b1", name), 8 * unit)
         for h in (0, 1):
             source = b_raw.at[3 * h + (d < 0)]
-            arrived(source, ("b1", h, name))
             device = at_row(0, d) if h == 0 else at_row(d, 0)
             part = pl.ds(u * unit, unit)
-            send(source.at[part], b_raw.at[3 * h + 2, part], ("b1", h, name + "2"), device)
+            send(source.at[part], b_raw.at[3 * h + 2, part], ("b1", "2"), device)
 
     def raw_pass(name, i):
         owner = raw_owner(PLACE[name])
         source = raw_half(owner, i)
-        arrived(source, ("raw", name, i))
+        arrived(("raw", name, i), RAW)
         if (name, i) == ("L", 0):
             send(source, source, ("raw", "L2", i), at_col(1))
         if (name, i) == ("R", 1):
             send(source, source, ("raw", "R2", i), at_col(-1))
-        send(source, source, ("rawP", PLACE[name], i), at_col(0, True))
+        send(source, source, ("rawP", PLACE[name]), at_col(0, True))
 
     raw_pass("L", 0)
     raw_pass("R", 1)
-    total = added(mine2, s2, copies2)
+    total = exchanged("row", 16, mine2, s2, 4)
     doubled = total / all_samples
     inverse = 1.0 / jnp.sqrt(doubled * (1.0 - 0.5 * doubled) + 0.1)
 
@@ -229,35 +216,34 @@
         b_part(h, df, 0)[...] = (scored(source[...]) * usable).astype(jnp.bfloat16)
         for name, d in (("L", 1), ("R", -1)):
             device = at_row(d, 0) if h == 0 else at_row(0, d)
-            send(b_part(h, df, 0), b_part(h, df, 0), ("b2", h, df, name), device)
+            send(b_part(h, df, 0), b_part(h, df, 0), ("b2", df), device)
 
     for h in (0, 1):
         b_score(h, 0, new_v.at[pl.ds(h * 2 * unit, 2 * unit)])
     for df in (-1, 1):
         for h in (0, 1):
             b_score(h, df, b_raw.at[3 * h + (df > 0)])
+    arrived(("b1", "2"), 8 * unit)
     for h in (0, 1):
-        for name, u in (("L2", 0), ("R2", 1)):
-            arrived(b_raw.at[3 * h + 2, pl.ds(u * unit, unit)], ("b1", h, name))
         b_score(h, 2, b_raw.at[3 * h + 2])
 
     def b_pass(df):
+        arrived(("b2", df), 8 * unit)
         for name, d, u in (("L", 1, 0), ("R", -1, 1)):
             for h in (0, 1):
-                arrived(b_part(h, df, PLACE[name]), ("b2", h, df, name))
                 source = b_part(h, df, PLACE[name], u, 1)
                 device = at_row(d, 0) if h == 0 else at_row(0, d)
-                send(source, source, ("b2", h, df, name + "2"), device)
+                send(source, source, ("b2", "2"), device)
 
     def a_pass(name, i):
         dx = PLACE[name]
         source = a_chunk(dx, False, i)
-        arrived(source, ("a", name, i))
+        arrived(("a", name, i), chunk)
         if name == "L" and i < half:
             send(source, rows_of(a_last, core * old_rows + RAW + i * chunk, chunk, 16), ("a", "L2", i), at_col(1))
         if name == "R" and i >= half:
             send(source, rows_of(a_last, core * old_rows + RAW + i * chunk, chunk, 16), ("a", "R2", i), at_col(-1))
-        send(source, source, ("aP", dx, i), at_col(0, True))
+        send(source, source, ("aP", dx), at_col(0, True))
 
     def raw_scored(dx, flip):
         a_rows(dx, flip, 0, RAW)[...] = scored(a_raw[raw_owner(dx, flip)]).astype(jnp.bfloat16)
@@ -266,87 +252,78 @@
     send(own_part, own_part, ("aP", 0), at_col(0, True))
     raw_pass("L", 1)
     raw_pass("R", 0)
-    arrived(a_raw.at[raw_owner(0, True)], ("rawP", 0))
+    arrived(("rawP", 0), 2 * RAW)
     raw_scored(0, True)
     raw_scored(-1, False)
     raw_scored(1, False)
     raw_pass("L2", 0)
     raw_pass("R2", 1)
     b_pass(0)
+    b_pass(-1)
     a_pass("L", 0)
     a_pass("R", half)
-    b_pass(-1)
-    a_pass("L", 1)
-    a_pass("R", half + 1)
     b_pass(1)
+    b_pass(2)
     raw_scored(2, False)
     for dx in (-1, 1, 2):
-        for i in (0, 1):
-            arrived(raw_half(raw_owner(dx, True), i), ("rawP", dx, i))
+        arrived(("rawP", dx), 2 * RAW)
         raw_scored(dx, True)
-    for i in range(half):
-        a_pass("L", half + i)
-        a_pass("R", i)
-        if i == 0:
-            b_pass(2)
     load_affected.wait()
     last_tile = (x + 2) % RING
     for j in range(2):
         scale_last[:, pl.ds(j * TILE, TILE)] = jnp.full(
             (8, TILE), affected[j, last_tile].astype(jnp.float32) * (1.0 / SNP)
         )
-    for df in (0, -1, 1, 2):
-        for name, u, place in (("L2", 0, -2), ("R2", 1, 2)):
-            for h in (0, 1):
-                arrived(b_part(h, df, place, u, 1), ("b2", h, df, name))
     load_grm.wait()
-
-    def update(dx, flip):
-        owner = raw_owner(dx, flip)
-        rows = pl.ds(pl.multiple_of(owner * old_rows, old_rows), old_rows)
+    for i in range(1, half):
+        a_pass("L", i)
+        a_pass("R", half + i)
+    for i in range(half - 1):
+        a_pass("L", half + i)
+        a_pass("R", i)
+    arrived(("b2", "2"), 16 * unit)
+    arrived(("aP", 0), old_rows - RAW)
+
+    def update(dx):
+        tile = (x + dx + RING) % RING
+        rows = pl.ds(pl.multiple_of(tile * TILE, TILE), TILE)
         for j in range(2):
             columns = pl.ds(j * TILE, TILE)
             product = contract(a_v[rows, :], b_v[columns, :])
-            scale = affected[j, owner * old_rows // TILE].astype(jnp.float32) * (1.0 / SNP)
+            scale = affected[j, tile].astype(jnp.float32) * (1.0 / SNP)
             out[rows, columns] = (
                 out[rows, columns].astype(jnp.float32) + product * scale
             ).astype(jnp.bfloat16)
 
-    update(0, False)
-    own_other = a_rows(0, True, RAW, old_rows - RAW)
-    arrived(own_other, ("aP", 0))
-    update(0, True)
-    update(-1, False)
+    a_pass("L", CHUNKS - 1)
+    a_pass("R", half - 1)
+    update(0)
+    arrived(("aP", -1), old_rows - RAW)
+    update(-1)
     for i in range(half):
-        if i < half - 1:
-            a_pass("L2", i)
-            a_pass("R2", half + i)
-    update(1, False)
-    for dx in (-1, 1):
-        for i in range(CHUNKS):
-            arrived(a_chunk(dx, True, i), ("aP", dx, i))
-        update(dx, True)
-    a_pass("L2", half - 1)
-    a_pass("R2", CHUNKS - 1)
-    for i in range(CHUNKS):
-        arrived(a_chunk(2, True, i), ("aP", 2, i))
-    for copy in sent:
-        copy.wait_send()
-    assert len(index) == COPIES, len(index)
+        a_pass("L2", i)
+        a_pass("R2", half + i)
+    arrived(("aP", 1), old_rows - RAW)
+    update(1)
+    arrived(("aP", 2), old_rows - RAW)
+    for group, rows in sent_rows.items():
+        target = out.at[pl.ds(0, rows)]
+        copy_of(target, target, "col", group, {"col": c}).wait_send()
+    for axis, size, slots, group in (("col", 8, s1, 3), ("row", 16, s2, 4)):
+        landed = slots.at[pl.ds(1, size - 1)]
+        copy_of(landed, landed, axis, group, {"col": c}).wait_send()
+    assert len(index) == ARRIVALS, len(index)
 
 
 def finish_kernel(updated, b_v, a_last, scale_last, result, last, store_sem):
     x = lax.axis_index("col") // 2
     rows = a_last.shape[0]
-    stores = []
 
     def store(source, start, count, columns):
         start = pl.multiple_of(start, count)
-        copy = pltpu.make_async_copy(
-            source, result.at[pl.ds(start, count), columns], store_sem.at[len(stores)]
-        )
-        copy.start()
-        stores.append(copy)
+        pltpu.make_async_copy(
+            source, result.at[pl.ds(start, count), columns], store_sem
+        ).start()
 
     whole = pl.ds(0, updated.shape[1])
     for d in (0, 1, 3):
@@ -363,8 +340,7 @@
                 updated[at, columns].astype(jnp.float32) + product * scale_last[0:1, columns]
             ).astype(jnp.bfloat16)
             store(last.at[pl.ds(i * piece, piece), columns], mine + i * piece, piece, columns)
-    for copy in stores:
-        copy.wait()
+    pltpu.make_async_copy(updated, result, store_sem).wait()
 
 
 def on_device(new_dosage, old_dosage, grm, counts, affected):
@@ -398,12 +374,8 @@
             vmem((8, 1, snps), jnp.float32),
             vmem((16, 1, snps), jnp.float32),
             dma((5,)),
-            dma((8,)),
-            dma((8,)),
-            dma((16,)),
-            dma((16,)),
-            dma((COPIES,)),
-            dma((COPIES,)),
+            dma((5,)),
+            dma((ARRIVALS,)),
         ],
         compiler_params=pltpu.CompilerParams(
             collective_id=0, has_side_effects=True, vmem_limit_bytes=40 * 1024 * 1024
@@ -415,7 +387,7 @@
         out_shape=jax.ShapeDtypeStruct(grm.shape, grm.dtype),
         in_specs=[vmem_spec] * 4,
         out_specs=hbm_spec,
-        scratch_shapes=[vmem((2 * old_rows, grm.shape[1]), grm.dtype), dma((7,))],
+        scratch_shapes=[vmem((2 * old_rows, grm.shape[1]), grm.dtype), dma(())],
         compiler_params=pltpu.CompilerParams(vmem_limit_bytes=16 * 1024 * 1024),
         name="finish",
     )(*[pltpu.with_memory_space_constraint(part, pltpu.VMEM) for part in parts])

time: 40 us -> 36.8 us (0.920)
  Pallas kernels: 39.8 us -> 36.7 us
    pallas_call x1, Pallas kernels: 37.8 us -> 34.7 us  [on_device(): pl.pallas_call(functools.partial(gather_kernel, float(old_rows * devices)...]
where the time goes in v4:
time: 36.8 us; the launch traced here: 36.7 us
  Pallas kernels  36.7 us (100%)
    pallas_call x1, Pallas kernels, on_device(): pl.pallas_call(functools.partial(gather_kernel, float(old_rows * devices)...  34.7 us
    pallas_call x1, Pallas kernels, on_device(): pl.pallas_call(finish_kernel, out_shape=jax.ShapeDtypeStruct(grm.shape, g...  2.03 us

profile of v4, /device:TPU:1, one launch (start us, length us, event | category | flops | bytes accessed | tf_op | source)
XLA Modules:
  0.0 36.7 jit_solution(9342730109898102088)
XLA Ops:
  0.0 34.7 %gather.1 = (bf16[2048,1024]{1,0:T(8,128)(2,1)S(1)}, bf16[1024,1024]{1,0:T(8,128)(2,1)S(1)}, bf16[512,1024]{1,0:T(8,128)(2,1)S(1)}, f32[8,1024]{1,0:T(8,128)S(1)}) custom-call(f32[256,1024]{1,0:T(8,128)} %old_hbm.1, f32[64,1024]{1,0:T(8,128)} %new_hbm.1, bf16[2048,1024]{1,0:T(8,128)(2,1)} %grm_hbm.1, s32[1,2]{1,0:T(1,128)} %bitcast.3, s32[2,4]{1,0:T(2,128)} %bitcast.2), custom_call_target="tpu_custom_call" | custom-call | tf_op jit(solution)/shard_map/gather/pallas_call | solution.py:354
  34.7 2.0 %finish.1 = bf16[2048,1024]{1,0:T(8,128)(2,1)} custom-call(bf16[2048,1024]{1,0:T(8,128)(2,1)S(1)} %get-tuple-element.9.updated, bf16[1024,1024]{1,0:T(8,128)(2,1)S(1)} %get-tuple-element.10.b_v, bf16[512,1024]{1,0:T(8,128)(2,1)S(1)} %get-tuple-element.11.a_last, f32[8,1024]{1,0:T(8,128)S(1)} %get-tuple-element.12.scale_last), custom_call_target="tpu_custom_call" | custom-call | tf_op jit(solution)/shard_map/finish/pallas_call | solution.py:385
